TPU v7x, 32 devices: a whole 2x2x4 slice. The times are simulated.
32 devices in a mesh: groups: 2 (over x), req: 16 (over z, y, core).
Axes of the slice: x: 2, y: 2, z: 4, core: 2. Of those that a mesh axis runs over, the one named last changes fastest.
Arguments:
- cache_states: bfloat16 [32, 16, 8192], P(('groups', 'req')), parts along dimension 0, may hold values from -6 to 6
- pool_keys: bfloat16 [512, 64, 512], P(('groups', 'req')), parts along dimension 0, may hold values from -64 to 64
- pool_values: bfloat16 [512, 64, 512], P(('groups', 'req')), parts along dimension 0, may hold values from -6 to 6
- slot_prefix: int32 [32], P('groups'), parts along dimension 0, may hold values from 0 to 15, each once
- page_table: int32 [32, 16], P('groups'), parts along dimension 0, may hold values from 0 to 15, each once within a row
- prefix_id: int32 [32], P('groups'), parts along dimension 0, may hold values from 0 to 15
- lengths: int32 [32], P(('groups', 'req')), parts along dimension 0, may hold values from 32 to 128, as said below
- queries: bfloat16 [4096, 4096], P(('groups', 'req')), parts along dimension 0, may hold values from -64 to 64
- suffix_keys: bfloat16 [4096, 512], P(('groups', 'req')), parts along dimension 0, may hold values from -6 to 6
- suffix_values: bfloat16 [4096, 512], P(('groups', 'req')), parts along dimension 0, may hold values from -6 to 6
- u_in: bfloat16 [4096, 8192], P(('groups', 'req')), parts along dimension 0, may hold values from -6 to 6
- dt_raw: bfloat16 [4096, 8192], P(('groups', 'req')), parts along dimension 0, may hold values from -3 to 3
- bc_in: float32 [32, 32, 128], P(('groups', 'req')), parts along dimension 0, may hold values from -6 to 6
- a_log: float32 [16, 8192], replicated, may hold values from 0 to 2.77
- dt_bias: float32 [8192], replicated, may hold values from -7 to -2.3
- d_skip: float32 [8192], replicated, may hold values from 0.5 to 1.5
Outputs:
- mamba_out: bfloat16 [4096, 8192], P(('groups', 'req')), parts along dimension 0
- attn_out: bfloat16 [4096, 4096], P(('groups', 'req')), parts along dimension 0
- final_state: float32 [32, 16, 8192], P(('groups', 'req')), parts along dimension 0
There are 2 independent parts, one for each index of `groups`. A program takes and returns all parts, laid end to end along the dimension named above; an argument that names none is the same for every part. Nothing has to cross between parts.
Inputs may be any that keep to these rules, and one draw needn't show every extreme that they name: `slot_prefix`: each prefix is held by exactly one slot. `page_table`: each row is a permutation of the local pages. `lengths`: some request has exactly 128 live tokens.
All inputs are finite; a program needn't handle non-finite values.
Results may differ from a plain program's by a relative error of at most 0.0049.
Values may be sent and summed in bfloat16 or wider, within the bound.
A program may use at most 128 MiB of HBM per device.

v0:
```python
import math

import jax
import jax.numpy as jnp
from jax import lax
from jax.sharding import PartitionSpec as P

QH = 32
KH = 4
HD = 128


token_block = 16


def selective_scan(start_state, u_rows, dt_rows, bc_rows, a_log, dt_bias, d_skip, length):
    token_count = u_rows.shape[0]
    nstate = a_log.shape[0]
    channels = u_rows.shape[1]
    rates = -jnp.exp(a_log)
    position = jnp.arange(token_count, dtype=jnp.int32)
    live_rows = (position < length).astype(jnp.float32)[:, None]
    deltas = jax.nn.softplus(dt_rows.astype(jnp.float32) + dt_bias[None, :]) * live_rows
    inputs = u_rows.astype(jnp.float32)
    b_rows = jnp.transpose(bc_rows[:nstate])
    c_rows = jnp.transpose(bc_rows[nstate:])
    blocks = token_count // token_block

    def advance(carried, blocked):
        delta_blk, input_blk, b_blk, c_blk = blocked
        emitted = []
        for offset in range(token_block):
            carried = (
                jnp.exp(delta_blk[offset][None, :] * rates) * carried
                + (delta_blk[offset] * input_blk[offset])[None, :] * b_blk[offset][:, None]
            )
            emitted.append(jnp.sum(c_blk[offset][:, None] * carried, axis=0))
        return (carried, jnp.stack(emitted))

    last_state, blocked_out = lax.scan(
        advance,
        start_state,
        (
            deltas.reshape(blocks, token_block, channels),
            inputs.reshape(blocks, token_block, channels),
            b_rows.reshape(blocks, token_block, nstate),
            c_rows.reshape(blocks, token_block, nstate),
        ),
    )
    outputs = blocked_out.reshape(token_count, channels) + d_skip[None, :] * inputs
    return ((outputs * live_rows).astype(jnp.bfloat16), last_state)


def attend(query_rows, prefix_keys, prefix_values, suffix_keys, suffix_values, length):
    row_count = query_rows.shape[0]
    q_group = QH // KH
    prefix_len = prefix_keys.shape[0]
    keys_all = jnp.concatenate([prefix_keys, suffix_keys], axis=0)
    values_all = jnp.concatenate([prefix_values, suffix_values], axis=0)
    position = jnp.arange(row_count, dtype=jnp.int32)
    key_pos = jnp.arange(prefix_len + row_count, dtype=jnp.int32) - prefix_len
    visible = (key_pos[None, :] <= position[:, None]) & (
        key_pos[None, :] > position[:, None] - prefix_len
    )
    score_scale = 1.0 / math.sqrt(HD)
    pieces = []
    for kv_head in range(KH):
        q_block = query_rows[:, kv_head * q_group * HD : (kv_head + 1) * q_group * HD].reshape(
            row_count * q_group, HD
        )
        k_block = keys_all[:, kv_head * HD : (kv_head + 1) * HD]
        scores = (
            lax.dot_general(
                q_block, k_block, (((1,), (1,)), ((), ())), preferred_element_type=jnp.float32
            )
            * score_scale
        )
        scores = scores.reshape(row_count, q_group, -1)
        scores = jnp.where(visible[:, None, :], scores, -1e30)
        highest = jnp.max(scores, axis=2, keepdims=True)
        exponent = jnp.exp(scores - highest)
        totals = jnp.sum(exponent, axis=2, keepdims=True)
        weights = (exponent / totals).astype(jnp.bfloat16).reshape(row_count * q_group, -1)
        mixed_rows = jnp.dot(
            weights,
            values_all[:, kv_head * HD : (kv_head + 1) * HD],
            preferred_element_type=jnp.float32,
        )
        pieces.append(mixed_rows.astype(jnp.bfloat16).reshape(row_count, q_group * HD))
    result = jnp.concatenate(pieces, axis=1)
    live_rows = (position < length)[:, None]
    return jnp.where(live_rows, result, jnp.zeros_like(result))


def local(
    cache_states,
    pool_keys,
    pool_values,
    slot_prefix,
    page_table,
    prefix_id,
    lengths,
    queries,
    suffix_keys,
    suffix_values,
    u_in,
    dt_raw,
    bc_in,
    a_log,
    dt_bias,
    d_skip,
):
    my_index = lax.axis_index("req")
    members = lax.axis_size("req")
    slot_count = slot_prefix.shape[0]
    matches = (slot_prefix[None, :] == prefix_id[:, None]).astype(jnp.int32)
    source = jnp.sum(matches * jnp.arange(slot_count, dtype=jnp.int32)[None, :], axis=1)
    kv_width = pool_keys.shape[2]
    page_order = page_table[slot_prefix[my_index]]
    ordered_keys = jnp.take(pool_keys, page_order, axis=0).reshape(1, -1, kv_width)
    ordered_values = jnp.take(pool_values, page_order, axis=0).reshape(1, -1, kv_width)
    nstate = cache_states.shape[1]
    channels = cache_states.shape[2]
    slice_width = channels // members
    state_rows = jnp.transpose(
        cache_states[0].reshape(nstate, members, slice_width), (1, 0, 2)
    ).reshape(1, members * nstate, slice_width)
    held_keys, held_values, held_states = (
        lax.all_to_all(ordered_keys, "req", split_axis=1, concat_axis=0, tiled=True),
        lax.all_to_all(ordered_values, "req", split_axis=1, concat_axis=0, tiled=True),
        lax.all_to_all(state_rows, "req", split_axis=1, concat_axis=0, tiled=True),
    )
    sent_keys = jnp.take(held_keys, source, axis=0)
    sent_values = jnp.take(held_values, source, axis=0)
    sent_states = jnp.take(held_states, source, axis=0)
    prefix_keys, prefix_values, picked_states = (
        lax.all_to_all(sent_keys, "req", split_axis=0, concat_axis=1, tiled=True),
        lax.all_to_all(sent_values, "req", split_axis=0, concat_axis=1, tiled=True),
        lax.all_to_all(sent_states, "req", split_axis=0, concat_axis=1, tiled=True),
    )
    start_state = (
        jnp.transpose(picked_states[0].reshape(members, nstate, slice_width), (1, 0, 2))
        .reshape(nstate, channels)
        .astype(jnp.float32)
    )
    length = lengths[0]
    mamba_out, last_state = selective_scan(
        start_state, u_in, dt_raw, bc_in[0], a_log, dt_bias, d_skip, length
    )
    attn_out = attend(queries, prefix_keys[0], prefix_values[0], suffix_keys, suffix_values, length)
    return (mamba_out, attn_out, last_state[None])


def solution(mesh):
    placed = (
        P(("groups", "req"), None, None),
        P(("groups", "req"), None, None),
        P(("groups", "req"), None, None),
        P("groups"),
        P("groups", None),
        P("groups"),
        P(("groups", "req")),
        P(("groups", "req"), None),
        P(("groups", "req"), None),
        P(("groups", "req"), None),
        P(("groups", "req"), None),
        P(("groups", "req"), None),
        P(("groups", "req"), None, None),
        P(),
        P(),
        P(),
    )
    return jax.shard_map(
        local,
        mesh=mesh,
        in_specs=placed,
        out_specs=(
            P(("groups", "req"), None),
            P(("groups", "req"), None),
            P(("groups", "req"), None, None),
        ),
        check_vma=False,
    )
```

profile of v0, /device:TPU:13, one launch (start us, length us, event | category | flops | bytes accessed | tf_op | source)
XLA Modules:
  0.0 305.6 jit_solution(16608789704047116486)
XLA Ops:
  0.7 1.2 copy.70
  3.0 2.2 reduce.8
  6.1 6.8 %all-to-all-start = ((bf16[16,2,4096]{2,1,0:T(2,128)(2,1)}), bf16[16,2,4096]{2,1,0:T(2,128)(2,1)S(1)}, u32[]{:S(2)}, u32[]{:S(2)}) async-start(bf16[16,2,4096]{2,1,0:T(2,128)(2,1)} %reshape.621), calls=%async_computation | async-start | bytes 524288 | tf_op jit(solution)/shard_map/all_to_all | solution.py:131
  14.9 1.2 dynamic_slice.20
  18.1 1.3 slice_bitcast_fusion
  22.5 1.8 gather_fusion.1
  26.4 1.6 copy.74
  28.0 8.1 %reduce.9 = bf16[1024,512]{1,0:T(8,128)(2,1)} reduce(bf16[1024,1,512]{2,1,0:T(2,128)(2,1)S(1)} %bitcast.330, bf16[]{:T(256)} %broadcast.204), dimensions={1}, to_apply=%bitcast.183.reduce_sub_computation | reduce | bytes 2097154
  36.1 2.8 reshape.625
  41.9 1.4 gather_fusion
  43.3 1.7 broadcast_select_fusion.4
  45.0 6.0 %all-to-all-start.1 = ((bf16[16,16,512]{2,1,0:T(8,128)(2,1)}), bf16[16,16,512]{2,1,0:T(8,128)(2,1)S(1)}, u32[]{:S(2)}, u32[]{:S(2)}) async-start(bf16[16,16,512]{2,1,0:T(8,128)(2,1)} %broadcast_select_fusion.4), calls=%async_computation.1 | async-start | bytes 524288 | tf_op jit(solution)/shard_map/all_to_all | solution.py:139
  51.0 1.5 broadcast_bitcast_fusion
  52.6 6.4 %all-to-all-done.1 = bf16[16,16,512]{2,1,0:T(8,128)(2,1)S(1)} async-done(((bf16[16,16,512]{2,1,0:T(8,128)(2,1)}), bf16[16,16,512]{2,1,0:T(8,128)(2,1)S(1)}, u32[]{:S(2)}, u32[]{:S(2)}) %all-to-all-start.1) | async-done | bytes 262176 | tf_op jit(solution)/shard_map/all_to_all | solution.py:139
  59.0 6.6 %all-to-all-start.4 = ((bf16[16,2,16384]{2,1,0:T(2,128)(2,1)}), bf16[16,2,16384]{2,1,0:T(2,128)(2,1)}, u32[]{:S(2)}, u32[]{:S(2)}) async-start(bf16[16,2,16384]{2,1,0:T(2,128)(2,1)} %reshape.625), calls=%async_computation.4 | async-start | bytes 2097152 | tf_op jit(solution)/shard_map/all_to_all | solution.py:130
  65.7 2.3 convert.7
  69.4 2.5 copy.61
  71.9 1.8 reshape.566
  73.7 2.9 copy.75
  76.7 8.1 %reduce.10 = bf16[1024,512]{1,0:T(8,128)(2,1)S(1)} reduce(bf16[1024,1,512]{2,1,0:T(2,128)(2,1)} %bitcast.329, bf16[]{:T(256)} %broadcast.204), dimensions={1}, to_apply=%bitcast.184.reduce_sub_computation | reduce | bytes 2097154
  84.8 2.0 reshape.623
  88.5 6.2 %fusion.32 = f32[128,8192]{1,0:T(8,128)} fusion(bf16[128,8192]{1,0:T(8,128)(2,1)} %param.31, f32[128]{0:T(128)S(1)} %get-tuple-element.202, f32[8192]{0:T(1024)S(1)} %copy-done.20), kind=kLoop, calls=%fused_computation.151 | loop fusion | flops 9437184 | bytes 6324736 | tf_op jit(solution)/shard_map/mul | solution.py:23
  94.8 6.1 %all-to-all-start.2 = ((bf16[16,2,16384]{2,1,0:T(2,128)(2,1)}), bf16[16,2,16384]{2,1,0:T(2,128)(2,1)}, u32[]{:S(2)}, u32[]{:S(2)}) async-start(bf16[16,2,16384]{2,1,0:T(2,128)(2,1)} %reshape.623), calls=%async_computation.2 | async-start | bytes 2097152 | tf_op jit(solution)/shard_map/all_to_all | solution.py:129
  101.0 5.8 %reshape.626 = bf16[1024,1,512]{2,1,0:T(2,128)(2,1)} reshape(bf16[16,2,16384]{2,1,0:T(2,128)(2,1)} %all-to-all-done.4) | data formatting | bytes 2097152
  106.8 1.9 copy.68
  108.7 17.1 %all-to-all-done.2 = bf16[16,2,16384]{2,1,0:T(2,128)(2,1)} async-done(((bf16[16,2,16384]{2,1,0:T(2,128)(2,1)}), bf16[16,2,16384]{2,1,0:T(2,128)(2,1)}, u32[]{:S(2)}, u32[]{:S(2)}) %all-to-all-start.2) | async-done | bytes 1048608 | tf_op jit(solution)/shard_map/all_to_all | solution.py:129
  125.8 5.8 %reshape.624 = bf16[1024,1,512]{2,1,0:T(2,128)(2,1)} reshape(bf16[16,2,16384]{2,1,0:T(2,128)(2,1)} %all-to-all-done.2) | data formatting | bytes 2097152
  131.6 2.9 copy.67
  134.5 1.7 gather_fusion.4
  136.2 2.0 gather_fusion.2
  138.2 2.8 broadcast_select_fusion
  141.0 4.8 %all-to-all-start.3 = ((bf16[16,64,512]{2,1,0:T(8,128)(2,1)}), bf16[16,64,512]{2,1,0:T(8,128)(2,1)}, u32[]{:S(2)}, u32[]{:S(2)}) async-start(bf16[16,64,512]{2,1,0:T(8,128)(2,1)} %get-tuple-element.190), calls=%async_computation.3 | async-start | bytes 2097152 | tf_op jit(solution)/shard_map/all_to_all | solution.py:137
  145.8 110.3 %while.12 = (s32[]{:T(128)}, f32[16,8192]{1,0:T(8,128)S(1)}, f32[8,16,8192]{2,1,0:T(8,128)}, f32[8,16,8192]{2,1,0:T(8,128)}, f32[16,8192]{1,0:T(8,128)S(1)}, /*i...) while((s32[]{:T(128)}, f32[16,8192]{1,0:T(8,128)S(1)}, ...), condition=%wide.region_18.19_spmd, body=%wide.region_1.18_spmd.sunk | while | flops 18874384 | bytes 15473949 | solution.py:40
  145.8 1.4 fusion.82
  147.2 5.2 %constant_dynamic-slice_fusion.65 = (f32[1,1,8192]{2,1,0:T(1,128)S(1)}, f32[1,1,8192]{2,1,0:T(1,128)S(1)}, f32[1,1,8192]{2,1,0:T(1,128)S(1)}, f32[1,1,8192]{2,1,...) fusion(f32[8,16,8192]{2,1,0:T(8,128)} %get-tuple-element.475, ...), kind=kLoop, calls=%fused_computation.82.clone.1 | loop fusion | bytes 2097216 | tf_op jit(solution)/shard_map/while/body/eval_jaxpr/slice | solution.py:35
  153.3 2.8 multiply_reduce_fusion.21
  159.8 1.3 fusion.82
  161.1 5.3 %constant_dynamic-slice_fusion.65 = (f32[1,1,8192]{2,1,0:T(1,128)S(1)}, f32[1,1,8192]{2,1,0:T(1,128)S(1)}, f32[1,1,8192]{2,1,0:T(1,128)S(1)}, f32[1,1,8192]{2,1,...) fusion(f32[8,16,8192]{2,1,0:T(8,128)} %get-tuple-element.475, ...), kind=kLoop, calls=%fused_computation.82.clone.1 | loop fusion | bytes 2097216 | tf_op jit(solution)/shard_map/while/body/eval_jaxpr/slice | solution.py:35
  167.3 2.8 multiply_reduce_fusion.21
  173.8 1.3 fusion.82
  175.1 5.1 %constant_dynamic-slice_fusion.65 = (f32[1,1,8192]{2,1,0:T(1,128)S(1)}, f32[1,1,8192]{2,1,0:T(1,128)S(1)}, f32[1,1,8192]{2,1,0:T(1,128)S(1)}, f32[1,1,8192]{2,1,...) fusion(f32[8,16,8192]{2,1,0:T(8,128)} %get-tuple-element.475, ...), kind=kLoop, calls=%fused_computation.82.clone.1 | loop fusion | bytes 2097216 | tf_op jit(solution)/shard_map/while/body/eval_jaxpr/slice | solution.py:35
  181.0 2.8 multiply_reduce_fusion.21
  187.6 1.3 fusion.82
  188.8 5.2 %constant_dynamic-slice_fusion.65 = (f32[1,1,8192]{2,1,0:T(1,128)S(1)}, f32[1,1,8192]{2,1,0:T(1,128)S(1)}, f32[1,1,8192]{2,1,0:T(1,128)S(1)}, f32[1,1,8192]{2,1,...) fusion(f32[8,16,8192]{2,1,0:T(8,128)} %get-tuple-element.475, ...), kind=kLoop, calls=%fused_computation.82.clone.1 | loop fusion | bytes 2097216 | tf_op jit(solution)/shard_map/while/body/eval_jaxpr/slice | solution.py:35
  194.9 2.8 multiply_reduce_fusion.21
  202.5 5.1 %constant_dynamic-slice_fusion.65 = (f32[1,1,8192]{2,1,0:T(1,128)S(1)}, f32[1,1,8192]{2,1,0:T(1,128)S(1)}, f32[1,1,8192]{2,1,0:T(1,128)S(1)}, f32[1,1,8192]{2,1,...) fusion(f32[8,16,8192]{2,1,0:T(8,128)} %get-tuple-element.475, ...), kind=kLoop, calls=%fused_computation.82.clone.1 | loop fusion | bytes 2097216 | tf_op jit(solution)/shard_map/while/body/eval_jaxpr/slice | solution.py:35
  208.5 2.8 multiply_reduce_fusion.21
  216.1 5.2 %constant_dynamic-slice_fusion.65 = (f32[1,1,8192]{2,1,0:T(1,128)S(1)}, f32[1,1,8192]{2,1,0:T(1,128)S(1)}, f32[1,1,8192]{2,1,0:T(1,128)S(1)}, f32[1,1,8192]{2,1,...) fusion(f32[8,16,8192]{2,1,0:T(8,128)} %get-tuple-element.475, ...), kind=kLoop, calls=%fused_computation.82.clone.1 | loop fusion | bytes 2097216 | tf_op jit(solution)/shard_map/while/body/eval_jaxpr/slice | solution.py:35
  222.1 2.8 multiply_reduce_fusion.21
  229.7 5.3 %constant_dynamic-slice_fusion.65 = (f32[1,1,8192]{2,1,0:T(1,128)S(1)}, f32[1,1,8192]{2,1,0:T(1,128)S(1)}, f32[1,1,8192]{2,1,0:T(1,128)S(1)}, f32[1,1,8192]{2,1,...) fusion(f32[8,16,8192]{2,1,0:T(8,128)} %get-tuple-element.475, ...), kind=kLoop, calls=%fused_computation.82.clone.1 | loop fusion | bytes 2097216 | tf_op jit(solution)/shard_map/while/body/eval_jaxpr/slice | solution.py:35
  235.9 2.8 multiply_reduce_fusion.21
  242.5 1.2 fusion.82
  243.7 5.0 %constant_dynamic-slice_fusion.65 = (f32[1,1,8192]{2,1,0:T(1,128)S(1)}, f32[1,1,8192]{2,1,0:T(1,128)S(1)}, f32[1,1,8192]{2,1,0:T(1,128)S(1)}, f32[1,1,8192]{2,1,...) fusion(f32[8,16,8192]{2,1,0:T(8,128)} %get-tuple-element.475, ...), kind=kLoop, calls=%fused_computation.82.clone.1 | loop fusion | bytes 2097216 | tf_op jit(solution)/shard_map/while/body/eval_jaxpr/slice | solution.py:35
  249.5 2.8 multiply_reduce_fusion.21
  256.1 6.3 %all-to-all-start.5 = ((bf16[16,64,512]{2,1,0:T(8,128)(2,1)}), bf16[16,64,512]{2,1,0:T(8,128)(2,1)S(1)}, u32[]{:S(2)}, u32[]{:S(2)}) async-start(bf16[16,64,512]{2,1,0:T(8,128)(2,1)} %get-tuple-element.189), calls=%async_computation.5 | async-start | bytes 2097152 | tf_op jit(solution)/shard_map/all_to_all | solution.py:138
  262.4 4.9 %fusion.34 = bf16[128,8192]{1,0:T(8,128)(2,1)} fusion(f32[8,16,8192]{2,1,0:T(8,128)} %get-tuple-element.47, f32[8192]{0:T(1024)} %param.35, f32[128]{0:T(128)S(1)} %get-tuple-element.202, bf16[128,8192]{1,0:T(8,128)(2,1)} %param.30), kind=kLoop, calls=%fused_computation.154 | loop fusion | flops 5242880 | bytes 8421888 | tf_op jit(solution)/shard_map/convert_element_type | solution.py:51
  267.3 1.9 fusion.73
  269.2 2.1 copy-done.3
  272.0 15.1 %all-to-all-done.5 = bf16[16,64,512]{2,1,0:T(8,128)(2,1)S(1)} async-done(((bf16[16,64,512]{2,1,0:T(8,128)(2,1)}), bf16[16,64,512]{2,1,0:T(8,128)(2,1)S(1)}, u32[]{:S(2)}, u32[]{:S(2)}) %all-to-all-start.5) | async-done | bytes 1048608 | tf_op jit(solution)/shard_map/all_to_all | solution.py:138
  288.1 3.3 %fusion.43 = bf16[1024,128]{1,0:T(8,128)(2,1)S(1)} fusion(f32[1024,1152]{0,1:T(8,128)} %copy-done.3, f32[1024]{0:T(1024)S(1)} %fusion.38, f32[1024]{0:T(1024)S(1)} %get-tuple-element.193, bf16[128,512]{1,0:T(8,128)(2,1)S(1)} %copy-done.24, bf16[1024,512]{1,0:T(8,128)(2,1)S(1)} %bitcast.379), kind=kOutput, calls=%fused_computation.170 | convolution fusion | flops 306249728 | bytes 6168576 | tf_op jit(solution)/shard_map/dot_general | solution.py:84
  291.5 1.9 fusion.74
  295.7 1.9 fusion.75
  300.0 1.9 fusion.76
  304.2 1.2 maximum_select_fusion
  (274 shorter events, 62.0 us)
Async XLA Ops:
  0.6 21.2 %copy-start = (bf16[16,64,512]{2,1,0:T(8,128)(2,1)S(1)}, bf16[16,64,512]{2,1,0:T(8,128)(2,1)}, u32[]{:S(2)}) copy-start(bf16[16,64,512]{2,1,0:T(8,128)(2,1)} %param.22) | copy-start | bytes 3145732
  0.6 18.7 %copy-start.11 = (bf16[128,4096]{1,0:T(8,128)(2,1)S(1)}, bf16[128,4096]{1,0:T(8,128)(2,1)}, u32[]{:S(2)}) copy-start(bf16[128,4096]{1,0:T(8,128)(2,1)} %param.27) | copy-start | bytes 3145732
  6.1 33.7 %all-to-all-start = ((bf16[16,2,4096]{2,1,0:T(2,128)(2,1)}), bf16[16,2,4096]{2,1,0:T(2,128)(2,1)S(1)}, u32[]{:S(2)}, u32[]{:S(2)}) async-start(bf16[16,2,4096]{2,1,0:T(2,128)(2,1)} %reshape.621), calls=%async_computation | async-start | bytes 524288 | tf_op jit(solution)/shard_map/all_to_all | solution.py:131
  36.1 29.5 %copy-start.4 = (bf16[128,8192]{1,0:T(8,128)(2,1)S(1)}, bf16[128,8192]{1,0:T(8,128)(2,1)}, u32[]{:S(2)}) copy-start(bf16[128,8192]{1,0:T(8,128)(2,1)} %param.30) | copy-start | bytes 6291460
  45.0 14.0 %all-to-all-start.1 = ((bf16[16,16,512]{2,1,0:T(8,128)(2,1)}), bf16[16,16,512]{2,1,0:T(8,128)(2,1)S(1)}, u32[]{:S(2)}, u32[]{:S(2)}) async-start(bf16[16,16,512]{2,1,0:T(8,128)(2,1)} %broadcast_select_fusion.4), calls=%async_computation.1 | async-start | bytes 524288 | tf_op jit(solution)/shard_map/all_to_all | solution.py:139
  52.6 15.4 %copy-start.22 = (f32[128,16]{0,1:T(8,128)S(1)}, f32[128,16]{0,1:T(8,128)}, u32[]{:S(2)}) copy-start(f32[128,16]{0,1:T(8,128)} %get-tuple-element.188) | copy-start | bytes 24580
  52.6 16.1 %copy-start.21 = (f32[128,16]{0,1:T(8,128)S(1)}, f32[128,16]{0,1:T(8,128)}, u32[]{:S(2)}) copy-start(f32[128,16]{0,1:T(8,128)} %get-tuple-element.187) | copy-start | bytes 24580
  59.0 9.0 %copy-start.9 = (bf16[16,16,512]{2,1,0:T(8,128)(2,1)}, bf16[16,16,512]{2,1,0:T(8,128)(2,1)S(1)}, u32[]{:S(2)}) copy-start(bf16[16,16,512]{2,1,0:T(8,128)(2,1)S(1)} %all-to-all-done.1) | copy-start | bytes 786436
  59.0 35.8 %all-to-all-start.4 = ((bf16[16,2,16384]{2,1,0:T(2,128)(2,1)}), bf16[16,2,16384]{2,1,0:T(2,128)(2,1)}, u32[]{:S(2)}, u32[]{:S(2)}) async-start(bf16[16,2,16384]{2,1,0:T(2,128)(2,1)} %reshape.625), calls=%async_computation.4 | async-start | bytes 2097152 | tf_op jit(solution)/shard_map/all_to_all | solution.py:130
  73.7 13.0 %copy-start.18 = (bf16[128,1024]{1,0:T(8,128)(2,1)S(1)}, bf16[128,1024]{1,0:T(8,128)(2,1)}, u32[]{:S(2)}) copy-start(bf16[128,1024]{1,0:T(8,128)(2,1)} %get-tuple-element.186) | copy-start | bytes 786436
  73.7 13.8 %copy-start.17 = (bf16[128,1024]{1,0:T(8,128)(2,1)S(1)}, bf16[128,1024]{1,0:T(8,128)(2,1)}, u32[]{:S(2)}) copy-start(bf16[128,1024]{1,0:T(8,128)(2,1)} %get-tuple-element.184) | copy-start | bytes 786436
  73.7 14.7 %copy-start.16 = (bf16[128,1024]{1,0:T(8,128)(2,1)S(1)}, bf16[128,1024]{1,0:T(8,128)(2,1)}, u32[]{:S(2)}) copy-start(bf16[128,1024]{1,0:T(8,128)(2,1)} %get-tuple-element.183) | copy-start | bytes 786436
  76.7 11.8 %copy-start.20 = (f32[8192]{0:T(1024)S(1)}, f32[8192]{0:T(1024)}, u32[]{:S(2)}) copy-start(f32[8192]{0:T(1024)} %param.34) | copy-start | bytes 98308
  88.5 12.3 %copy-start.19 = (f32[16,8192]{1,0:T(8,128)S(1)}, f32[16,8192]{1,0:T(8,128)}, u32[]{:S(2)}) copy-start(f32[16,8192]{1,0:T(8,128)} %param.33) | copy-start | bytes 1572868
  88.5 12.4 %copy-start.10 = (bf16[16,16,512]{2,1,0:T(8,128)(2,1)S(1)}, bf16[16,16,512]{2,1,0:T(8,128)(2,1)}, u32[]{:S(2)}) copy-start(bf16[16,16,512]{2,1,0:T(8,128)(2,1)} %copy-done.9) | copy-start | bytes 786436
  94.8 31.0 %all-to-all-start.2 = ((bf16[16,2,16384]{2,1,0:T(2,128)(2,1)}), bf16[16,2,16384]{2,1,0:T(2,128)(2,1)}, u32[]{:S(2)}, u32[]{:S(2)}) async-start(bf16[16,2,16384]{2,1,0:T(2,128)(2,1)} %reshape.623), calls=%async_computation.2 | async-start | bytes 2097152 | tf_op jit(solution)/shard_map/all_to_all | solution.py:129
  131.5 6.6 %copy-start.23 = (pred[16]{0:T(512)(128)(4,1)S(1)}, pred[16]{0:T(512)(128)(4,1)}, u32[]{:S(2)}) copy-start(pred[16]{0:T(512)(128)(4,1)} %compare_and_fusion.1) | copy-start | bytes 52
  141.0 115.1 %all-to-all-start.3 = ((bf16[16,64,512]{2,1,0:T(8,128)(2,1)}), bf16[16,64,512]{2,1,0:T(8,128)(2,1)}, u32[]{:S(2)}, u32[]{:S(2)}) async-start(bf16[16,64,512]{2,1,0:T(8,128)(2,1)} %get-tuple-element.190), calls=%async_computation.3 | async-start | bytes 2097152 | tf_op jit(solution)/shard_map/all_to_all | solution.py:137
  256.1 11.2 %copy-start.2 = (f32[16,8192]{1,0:T(8,128)}, f32[16,8192]{1,0:T(8,128)S(1)}, u32[]{:S(2)}) copy-start(f32[16,8192]{1,0:T(8,128)S(1)} %get-tuple-element.48) | copy-start | bytes 1572868
  256.1 31.0 %all-to-all-start.5 = ((bf16[16,64,512]{2,1,0:T(8,128)(2,1)}), bf16[16,64,512]{2,1,0:T(8,128)(2,1)S(1)}, u32[]{:S(2)}, u32[]{:S(2)}) async-start(bf16[16,64,512]{2,1,0:T(8,128)(2,1)} %get-tuple-element.189), calls=%async_computation.5 | async-start | bytes 2097152 | tf_op jit(solution)/shard_map/all_to_all | solution.py:138
  262.4 4.9 %copy-start.5 = (bf16[128,512]{1,0:T(8,128)(2,1)S(1)}, bf16[128,512]{1,0:T(8,128)(2,1)}, u32[]{:S(2)}) copy-start(bf16[128,512]{1,0:T(8,128)(2,1)} %param.28) | copy-start | bytes 393220
  262.4 4.9 %copy-start.8 = (bf16[1024,128]{1,0:T(8,128)(2,1)S(1)}, bf16[1024,128]{1,0:T(8,128)(2,1)}, u32[]{:S(2)}) copy-start(bf16[1024,128]{1,0:T(8,128)(2,1)} %reshape.566) | copy-start | bytes 786436
  269.2 2.1 copy-start.3
  269.2 18.9 %copy-start.24 = (bf16[128,512]{1,0:T(8,128)(2,1)S(1)}, bf16[128,512]{1,0:T(8,128)(2,1)}, u32[]{:S(2)}) copy-start(bf16[128,512]{1,0:T(8,128)(2,1)} %param.29) | copy-start | bytes 393220
  287.1 1.0 copy-start.12
  288.1 3.4 %copy-start.7 = (bf16[1024,128]{1,0:T(8,128)(2,1)S(1)}, bf16[1024,128]{1,0:T(8,128)(2,1)}, u32[]{:S(2)}) copy-start(bf16[1024,128]{1,0:T(8,128)(2,1)} %reshape.564) | copy-start | bytes 786436
  293.4 1.2 copy-start.13
  294.7 1.1 copy-start.6
  297.7 1.2 copy-start.14
  301.9 1.2 copy-start.15
  301.9 1.2 copy-start.25
  303.1 2.3 copy-start.1
where the time goes:
time: 311 us; the launch traced here: 306 us
  local copies, waits for them, and re-layouts  120 us (39%)
  other arithmetic  91.2 us (29%)
  waiting for transfers between devices  38.6 us (12%)
  starting transfers between devices  36.6 us (12%)
  matrix products  13.7 us (4%)
  between operations  3.9 us (1%)
    reduce_sum x40, other arithmetic, advance(): emitted.append(jnp.sum(c_blk[offset][:, None] * carried, axis=0))  44.2 us
    slice x8, local copies, waits for them, and re-layouts, advance(): input_blk[offset]  41.5 us
    unnamed x63, local copies, waits for them, and re-layouts  30.5 us
    unnamed x4, other arithmetic  18.4 us
    all_to_all x1, waiting for transfers between devices, local(): lax.all_to_all(ordered_keys, 'req', split_axis=1, concat_axis=0, tiled=True)  17.1 us
    all_to_all x1, waiting for transfers between devices, local(): lax.all_to_all(sent_values, 'req', split_axis=0, concat_axis=1, tiled=True)  15.1 us
    mul x8, local copies, waits for them, and re-layouts, advance(): (delta_blk[offset] * input_blk[offset])[None, :] * b_blk[offset][:, None]  9.46 us
    dot_general x4, matrix products, attend(): lax.dot_general(q_block, k_block, (((1,), (1,)), ((), ())), preferred_ele...  7.66 us
  transfers between devices with their start and end apart: 6, of which 3 were waited for; matrix products, arithmetic and copies ran while one was open for 59% of the time, Pallas kernels for 0%

commit v1 on v0

v1 whole, which is shorter than its diff:
```python
import functools
import math

import jax
import jax.numpy as jnp
from jax import lax
from jax.experimental import pallas as pl
from jax.experimental.pallas import tpu as pltpu
from jax.sharding import PartitionSpec as P

HD = 128
MESH = pl.DeviceIdType.MESH
LOG2E = 1.4426950408889634
SUB = 8
LANE = 128
WIDE = SUB * LANE


def kernel(
    n,
    source,
    chunk_order,
    lengths,
    bc_cols,
    dt_bias,
    d_skip,
    cache,
    pool_k,
    pool_v,
    q_hbm,
    sk_hbm,
    sv_hbm,
    u_hbm,
    dt_hbm,
    a_hbm,
    mamba_hbm,
    attn_hbm,
    final_hbm,
    held_s,
    held_k,
    held_v,
    send_s,
    send_k,
    send_v,
    got_s,
    got_k,
    got_v,
    keys,
    values,
    q_v,
    u_v,
    dt_v,
    a_v,
    mamba_v,
    attn_v,
    final_v,
    delta_w,
    du_w,
    y_w,
    h_w,
    rate_w,
    bc_w,
    w_w,
    inv_w,
    send_sem,
    recv_sem,
    own_sem,
    in_sem,
    out_sem,
):
    me = lax.axis_index("req")
    tokens, channels = u_v.shape
    nstate = a_v.shape[0]
    blocks = channels // WIDE
    width = held_s.shape[2]
    total = keys.shape[0]
    prefix_len = total - tokens
    chunks, size, _ = got_k.shape
    per = chunks // n
    heads = q_v.shape[1] // HD
    q_group = heads // (keys.shape[1] // HD)

    loads = [
        pltpu.make_async_copy(dt_hbm, dt_v, in_sem.at[0]),
        pltpu.make_async_copy(u_hbm, u_v, in_sem.at[1]),
        pltpu.make_async_copy(a_hbm, a_v, in_sem.at[2]),
        pltpu.make_async_copy(q_hbm, q_v, in_sem.at[3]),
        pltpu.make_async_copy(sk_hbm, keys.at[pl.ds(prefix_len, tokens)], in_sem.at[4]),
        pltpu.make_async_copy(sv_hbm, values.at[pl.ds(prefix_len, tokens)], in_sem.at[5]),
    ]
    for load in loads:
        load.start()

    barrier = pltpu.get_barrier_semaphore()

    def greet(d, c):
        peer = lax.rem(me + d, n)
        pl.semaphore_signal(barrier, inc=1, device_id={"req": peer}, device_id_type=MESH)
        return c

    lax.fori_loop(1, n, greet, 0)
    pl.semaphore_wait(barrier, n - 1)

    def part(kind, index):
        if kind == 0:
            return cache.at[:, pl.ds(pl.multiple_of(index * width, width), width)]
        pool = pool_k if kind == 1 else pool_v
        return pool.at[pl.ds(index * per, per)]

    held = (held_s, held_k, held_v)
    outgoing = (send_s, send_k, send_v)
    got = (got_s, got_k, got_v)

    def spread(kind):
        own = pltpu.make_async_copy(part(kind, me), held[kind].at[me], own_sem.at[kind])
        own.start()

        def step(d, c):
            peer = lax.rem(me + d, n)
            pltpu.make_async_remote_copy(
                src_ref=part(kind, peer),
                dst_ref=held[kind].at[me],
                send_sem=send_sem.at[kind],
                recv_sem=recv_sem.at[kind],
                device_id={"req": peer},
                device_id_type=MESH,
            ).start()
            return c

        lax.fori_loop(1, n, step, 0)

    def settle(ref, sem):
        piece = ref.at[pl.ds(0, ref.shape[0] // n * (n - 1))]
        pltpu.make_async_copy(piece, piece, sem).wait()

    def collect(kind):
        settle(held[kind], recv_sem.at[kind])
        pltpu.make_async_copy(part(kind, me), held[kind].at[me], own_sem.at[kind]).wait()

        def pick(r, c):
            outgoing[kind][r] = held[kind][source[r]]
            return c

        lax.fori_loop(0, n, pick, 0)
        landing = got_s.at[me] if kind == 0 else got[kind].at[pl.ds(me * per, per)]
        if kind == 0:
            got_s[me] = held_s[source[me]]
        else:
            got[kind][pl.ds(me * per, per)] = held[kind][source[me]]

        def step(d, c):
            peer = lax.rem(me + d, n)
            pltpu.make_async_remote_copy(
                src_ref=outgoing[kind].at[peer],
                dst_ref=landing,
                send_sem=send_sem.at[3 + kind],
                recv_sem=recv_sem.at[3 + kind],
                device_id={"req": peer},
                device_id_type=MESH,
            ).start()
            return c

        lax.fori_loop(1, n, step, 0)

    spread(0)
    spread(1)

    def widen(k, c):
        column = jnp.broadcast_to(bc_cols[k], (tokens, LANE))
        for s in range(SUB):
            bc_w[k, pl.ds(s, tokens, stride=SUB), :] = column
        return c

    lax.fori_loop(0, 2 * nstate, widen, 0)

    length = lengths[0]
    live = lax.broadcasted_iota(jnp.int32, (tokens, LANE), 0) < length
    loads[0].wait()
    loads[1].wait()

    def steps_of(b, c):
        for s in range(SUB):
            at = pl.ds(pl.multiple_of(b * WIDE + s * LANE, LANE), LANE)
            raw = dt_v[:, at].astype(jnp.float32) + dt_bias[:, at]
            soft = jnp.maximum(raw, 0.0) + jnp.log1p(jnp.exp(-jnp.abs(raw)))
            delta = jnp.where(live, soft, 0.0)
            delta_w[b, pl.ds(s, tokens, stride=SUB), :] = delta
            du_w[b, pl.ds(s, tokens, stride=SUB), :] = delta * u_v[:, at].astype(jnp.float32)
        return c

    lax.fori_loop(0, blocks, steps_of, 0)
    collect(0)
    spread(2)
    loads[2].wait()

    def rates_of(b, c):
        for s in range(SUB):
            at = pl.ds(pl.multiple_of(b * WIDE + s * LANE, LANE), LANE)
            rate_w[b, pl.ds(s, nstate, stride=SUB), :] = -LOG2E * jnp.exp(a_v[:, at])
        return c

    lax.fori_loop(0, blocks, rates_of, 0)
    collect(1)
    settle(got_s, recv_sem.at[3])

    def scan_block(b, c):
        for s in range(SUB):
            first = b * WIDE + s * LANE
            inside = lax.rem(first, width)
            start = got_s[lax.div(first, width), :, pl.ds(pl.multiple_of(inside, LANE), LANE)]
            h_w[pl.ds(s, nstate, stride=SUB), :] = start.astype(jnp.float32)
        rates = [rate_w[b, pl.ds(k * SUB, SUB), :] for k in range(nstate)]

        def advance(t, hs):
            at = pl.ds(pl.multiple_of(t * SUB, SUB), SUB)
            delta = delta_w[b, at, :]
            du = du_w[b, at, :]
            new = []
            sums = [None, None]
            for k in range(nstate):
                h = jnp.exp2(delta * rates[k]) * hs[k] + du * bc_w[k, at, :]
                term = bc_w[nstate + k, at, :] * h
                sums[k % 2] = term if sums[k % 2] is None else sums[k % 2] + term
                new.append(h)
            y_w[at, :] = sums[0] + sums[1]
            return tuple(new)

        def pair(i, hs):
            return advance(2 * i + 1, advance(2 * i, hs))

        hs = tuple(h_w[pl.ds(k * SUB, SUB), :] for k in range(nstate))
        hs = lax.fori_loop(0, tokens // 2, pair, hs)
        for k in range(nstate):
            h_w[pl.ds(k * SUB, SUB), :] = hs[k]
        for s in range(SUB):
            at = pl.ds(pl.multiple_of(b * WIDE + s * LANE, LANE), LANE)
            final_v[:, at] = h_w[pl.ds(s, nstate, stride=SUB), :]
            y = y_w[pl.ds(s, tokens, stride=SUB), :] + d_skip[:, at] * u_v[:, at].astype(jnp.float32)
            mamba_v[:, at] = jnp.where(live, y, 0.0).astype(jnp.bfloat16)
        return c

    half = blocks // 2
    lax.fori_loop(0, half, scan_block, 0)
    collect(2)
    lax.fori_loop(half, blocks, scan_block, 0)

    stores = [
        pltpu.make_async_copy(mamba_v, mamba_hbm, out_sem.at[0]),
        pltpu.make_async_copy(final_v, final_hbm, out_sem.at[1]),
        pltpu.make_async_copy(attn_v, attn_hbm, out_sem.at[2]),
    ]
    stores[0].start()
    stores[1].start()

    def order(kind, into):
        def step(k, c):
            to = pl.ds(pl.multiple_of(k * size, size), size)
            into[to, :] = got[kind][chunk_order[k]]
            return c

        lax.fori_loop(0, chunks, step, 0)

    loads[3].wait()
    loads[4].wait()
    settle(got_k, recv_sem.at[4])
    order(1, keys)
    factor = LOG2E / math.sqrt(HD)
    row = lax.broadcasted_iota(jnp.int32, (tokens, tokens), 0)
    col = lax.broadcasted_iota(jnp.int32, (tokens, tokens), 1)

    def weigh(j):
        g = lax.div(j, q_group)
        q = q_v[:, pl.ds(pl.multiple_of(j * HD, HD), HD)]
        k = keys[:, pl.ds(pl.multiple_of(g * HD, HD), HD)]
        scores = lax.dot_general(q, k, (((1,), (1,)), ((), ())), preferred_element_type=jnp.float32)
        scores = jnp.concatenate(
            [
                jnp.where(col > row, scores[:, :tokens], -1e30),
                scores[:, tokens:prefix_len],
                jnp.where(col <= row, scores[:, prefix_len:], -1e30),
            ],
            axis=1,
        )
        highest = jnp.max(scores, axis=1, keepdims=True)
        weight = jnp.exp2((scores - highest) * factor)
        inv_w[j] = jnp.broadcast_to(1.0 / jnp.sum(weight, axis=1, keepdims=True), (tokens, HD))
        w_w[j] = weight.astype(jnp.bfloat16)

    def weigh_pair(i, c):
        weigh(2 * i)
        weigh(2 * i + 1)
        return c

    lax.fori_loop(0, heads // 2, weigh_pair, 0)

    loads[5].wait()
    settle(got_v, recv_sem.at[5])
    order(2, values)

    def mix(j):
        g = lax.div(j, q_group)
        v = values[:, pl.ds(pl.multiple_of(g * HD, HD), HD)]
        out = jnp.dot(w_w[j], v, preferred_element_type=jnp.float32) * inv_w[j]
        out = jnp.where(live, out, 0.0)
        attn_v[:, pl.ds(pl.multiple_of(j * HD, HD), HD)] = out.astype(jnp.bfloat16)

    def mix_pair(i, c):
        mix(2 * i)
        mix(2 * i + 1)
        return c

    lax.fori_loop(0, heads // 2, mix_pair, 0)
    stores[2].start()
    for kind in range(3):
        settle(held[kind], send_sem.at[kind])
        settle(outgoing[kind], send_sem.at[3 + kind])
    for store in stores:
        store.wait()


def solution(mesh):
    n = mesh.shape["req"]

    def local(
        cache_states,
        pool_keys,
        pool_values,
        slot_prefix,
        page_table,
        prefix_id,
        lengths,
        queries,
        suffix_keys,
        suffix_values,
        u_in,
        dt_raw,
        bc_in,
        a_log,
        dt_bias,
        d_skip,
    ):
        nstate, channels = a_log.shape
        tokens = u_in.shape[0]
        kv = suffix_keys.shape[1]
        prefix_len = pool_keys.shape[0] * pool_keys.shape[1]
        heads = queries.shape[1] // HD
        page = pool_keys.shape[1]
        size = min(page, prefix_len // n)
        chunks = prefix_len // size
        per = chunks // n
        me = lax.axis_index("req")
        slots = jnp.arange(n, dtype=jnp.int32)
        source = jnp.sum(jnp.where(slot_prefix[None] == prefix_id[:, None], slots[None], 0), axis=1)
        pages = page_table[prefix_id[me]]
        inner = jnp.arange(page // size, dtype=jnp.int32)
        chunk_order = (pages[:, None] * (page // size) + inner[None]).reshape(-1)
        width = channels // n
        blocks = channels // WIDE
        bf, f32 = jnp.bfloat16, jnp.float32
        smem = pl.BlockSpec(memory_space=pltpu.SMEM)
        vmem = pl.BlockSpec(memory_space=pltpu.VMEM)
        hbm = pl.BlockSpec(memory_space=pl.ANY)
        total = prefix_len + tokens
        scratch = (
            ([pltpu.VMEM((n, nstate, width), bf)] + [pltpu.VMEM((n, per, size, kv), bf)] * 2) * 2
            + [pltpu.VMEM((n, nstate, width), bf)] + [pltpu.VMEM((chunks, size, kv), bf)] * 2
            + [
                pltpu.VMEM((total, kv), bf),
                pltpu.VMEM((total, kv), bf),
                pltpu.VMEM(queries.shape, bf),
                pltpu.VMEM(u_in.shape, bf),
                pltpu.VMEM(dt_raw.shape, bf),
                pltpu.VMEM(a_log.shape, f32),
                pltpu.VMEM(u_in.shape, bf),
                pltpu.VMEM(queries.shape, bf),
                pltpu.VMEM(a_log.shape, f32),
                pltpu.VMEM((blocks, tokens * SUB, LANE), f32),
                pltpu.VMEM((blocks, tokens * SUB, LANE), f32),
                pltpu.VMEM((tokens * SUB, LANE), f32),
                pltpu.VMEM((nstate * SUB, LANE), f32),
                pltpu.VMEM((blocks, nstate * SUB, LANE), f32),
                pltpu.VMEM((2 * nstate, tokens * SUB, LANE), f32),
                pltpu.VMEM((heads, tokens, total), bf),
                pltpu.VMEM((heads, tokens, HD), f32),
                pltpu.SemaphoreType.DMA((6,)),
                pltpu.SemaphoreType.DMA((6,)),
                pltpu.SemaphoreType.DMA((3,)),
                pltpu.SemaphoreType.DMA((6,)),
                pltpu.SemaphoreType.DMA((3,)),
            ]
        )
        mamba, attn, final = pl.pallas_call(
            functools.partial(kernel, n),
            out_shape=(
                jax.ShapeDtypeStruct(u_in.shape, bf),
                jax.ShapeDtypeStruct(queries.shape, bf),
                jax.ShapeDtypeStruct(a_log.shape, f32),
            ),
            in_specs=[smem] * 3 + [vmem] * 3 + [hbm] * 9,
            out_specs=(hbm, hbm, hbm),
            scratch_shapes=scratch,
            compiler_params=pltpu.CompilerParams(
                collective_id=0, has_side_effects=True, vmem_limit_bytes=64 * 1000 * 1024
            ),
        )(
            source,
            chunk_order,
            lengths,
            bc_in[0][:, :, None],
            dt_bias[None],
            d_skip[None],
            cache_states[0],
            pool_keys.reshape(chunks, size, kv),
            pool_values.reshape(chunks, size, kv),
            queries,
            suffix_keys,
            suffix_values,
            u_in,
            dt_raw,
            a_log,
        )
        return mamba, attn, final[None]

    split = ("groups", "req")
    one, two, three = P(split), P(split, None), P(split, None, None)
    return jax.shard_map(
        local,
        mesh=mesh,
        in_specs=(
            three,
            three,
            three,
            P("groups"),
            P("groups", None),
            P("groups"),
            one,
            two,
            two,
            two,
            two,
            two,
            three,
            P(),
            P(),
            P(),
        ),
        out_specs=(two, two, three),
        check_vma=False,
    )
```

time: 311 us -> 130 us (0.42); the launches traced: 306 us -> 129 us
  Pallas kernels: 0 us -> 115 us
  local copies, waits for them, and re-layouts: 120 us -> 9.82 us
  other arithmetic: 91.2 us -> 1.36 us
  waiting for transfers between devices: 38.6 us -> 0 us
  starting transfers between devices: 36.6 us -> 0 us
  matrix products: 13.7 us -> 0 us
    pallas_call x0 -> x1, Pallas kernels: none -> 115 us  [local(): pl.pallas_call(functools.partial(kernel, n), out_shape=(jax.ShapeDtypeStr...]
    reduce_sum x45 -> x1, other arithmetic: 47.8 us -> 1.36 us  [local(): jnp.sum(jnp.where(slot_prefix[None] == prefix_id[:, None], slots[None], 0...]
    slice x9 -> x0, local copies, waits for them, and re-layouts: 42.6 us -> none  [the longest x8 41.5 us: advance(): input_blk[offset]]
    all_to_all x6 -> x0, waiting for transfers between devices: 38.6 us -> none  [the longest x1 17.1 us: local(): lax.all_to_all(ordered_keys, 'req', split_axis=1, concat_axis=0, tiled=True)]
    all_to_all x6 -> x0, starting transfers between devices: 36.6 us -> none  [the longest x1 6.78 us: local(): lax.all_to_all(state_rows, 'req', split_axis=1, concat_axis=0, tiled=True)]
    unnamed x63 -> x9, local copies, waits for them, and re-layouts: 30.5 us -> 5.39 us
    unnamed x4 -> x0, other arithmetic: 18.4 us -> none
    dot_general x8 -> x0, matrix products: 13.7 us -> none  [the longest x4 7.66 us: attend(): lax.dot_general(q_block, k_block, (((1,), (1,)), ((), ())), preferred_ele...]
  transfers between devices with their start and end apart: 6 -> 0, of which waited for: 3 -> 0; matrix products, arithmetic and copies ran while one was open for 59% -> 0% of each run, Pallas kernels for 0% -> 0%
where the time goes in v1:
time: 130 us; the launch traced here: 129 us
  Pallas kernels  115 us (88%)
  local copies, waits for them, and re-layouts  9.82 us (8%)
  between operations  3.27 us (3%)
  other arithmetic  1.36 us (1%)
    pallas_call x1, Pallas kernels, local(): pl.pallas_call(functools.partial(kernel, n), out_shape=(jax.ShapeDtypeStr...  115 us
    unnamed x9, local copies, waits for them, and re-layouts  5.39 us
    another operation x1, local copies, waits for them, and re-layouts, local(): bc_in[0][:, :, None]  2.68 us

profile of v1, /device:TPU:13, one launch (start us, length us, event | category | flops | bytes accessed | tf_op | source)
XLA Modules:
  0.0 129.2 jit_solution(14255696970004821231)
XLA Ops:
  0.6 0.0 copy-start
  1.3 1.2 dynamic_slice.6
  4.5 0.0 copy-done
  4.5 0.5 dynamic-slice_bitcast_fusion.chunk_order
  5.0 1.4 %select_reduce_fusion.source = s32[16]{0:T(128)} fusion(s32[16]{0:T(128)} %param.19, s32[16]{0:T(128)} %param.21), kind=kLoop, calls=%fused_computation | loop fusion | flops 752 | bytes 192 | tf_op jit(solution)/shard_map/reduce_sum | solution.py:353
  6.4 2.7 %copy.20.bc_cols = f32[32,128,1]{2,1,0:T(8,128)} copy(f32[32,128,1]{1,0,2:T(8,128)} %bitcast.12) | data formatting | bytes 32768 | tf_op jit(solution)/shard_map/broadcast_in_dim;squeeze | solution.py:409
  9.1 114.8 %shard_map.175 = (bf16[128,8192]{1,0:T(8,128)(2,1)}, bf16[128,4096]{1,0:T(8,128)(2,1)}, f32[16,8192]{1,0:T(8,128)}) custom-call(s32[16]{0:T(128)} %select_reduce_fusion.source, s32[16]{0:T(128)} %dynamic-slice_bitcast_fusion.chunk_order, s32[1]{0:T(128)S(6)} %copy.24.lengths, f32[32,128,1]{2,1,0:T(8,128)} %copy.20.bc_cols, f32[1,8192]{1,0:T(1,128)} %bitcast.10, ...), custom_call_target="tpu_custom_call" | custom-call | tf_op jit(solution)/shard_map/pallas_call | solution.py:392
  123.8 0.0 copy-start.1
  123.9 3.2 %copy.25 = bf16[128,8192]{1,0:T(8,128)(2,1)} copy(bf16[128,8192]{1,0:T(8,128)(2,1)} %get-tuple-element.12) | data formatting | bytes 4194304
  127.0 0.0 copy-done.1
  127.0 0.0 copy-start.2
  127.0 1.0 copy.26
  128.0 0.4 copy-done.2
  128.4 0.8 copy.27
Async XLA Ops:
  0.6 3.9 %copy-start = (s32[16,16]{1,0:T(8,128)S(1)}, s32[16,16]{1,0:T(8,128)}, u32[]{:S(2)}) copy-start(s32[16,16]{1,0:T(8,128)} %param.20) | copy-start | bytes 3076
  123.8 3.2 %copy-start.1 = (bf16[128,4096]{1,0:T(8,128)(2,1)S(1)}, bf16[128,4096]{1,0:T(8,128)(2,1)}, u32[]{:S(2)}) copy-start(bf16[128,4096]{1,0:T(8,128)(2,1)} %get-tuple-element.13) | copy-start | bytes 3145732
  127.0 1.4 %copy-start.2 = (f32[16,8192]{1,0:T(8,128)S(1)}, f32[16,8192]{1,0:T(8,128)}, u32[]{:S(2)}) copy-start(f32[16,8192]{1,0:T(8,128)} %get-tuple-element.8) | copy-start | bytes 1572868

commit v2 on v1

v2 whole, which is shorter than its diff:
```python
import functools
import math

import jax
import jax.numpy as jnp
from jax import lax
from jax.experimental import pallas as pl
from jax.experimental.pallas import tpu as pltpu
from jax.sharding import PartitionSpec as P

HD = 128
MESH = pl.DeviceIdType.MESH
LOG2E = 1.4426950408889634
SUB = 8
LANE = 128
WIDE = SUB * LANE
CAPS = (3, 4, 5)


def plan_kernel(
    n, w, slot_prefix, prefix_id, page_table, where_ref, source, order, right, left, final, need, far_r, far_l, before
):
    me = where_ref[0]
    p = me // w
    planes = n // w

    def clear(s, c):
        far_r[s] = -1
        far_l[s] = n
        return c

    lax.fori_loop(0, n, clear, 0)

    def invert(s, c):
        before[slot_prefix[s]] = s
        return c

    lax.fori_loop(0, n, invert, 0)

    def find(r, c):
        s = before[prefix_id[r]]
        source[r] = s
        far_r[s] = jnp.maximum(far_r[s], r // w)
        far_l[s] = jnp.minimum(far_l[s], r // w)
        return c

    lax.fori_loop(0, n, find, 0)

    def pages(k, c):
        order[k] = page_table[prefix_id[me], k]
        return c

    lax.fori_loop(0, page_table.shape[1], pages, 0)

    def start(k, c):
        for ref in (right, left):
            ref[0, k] = 0
            ref[1, k] = -1
        return c

    lax.fori_loop(0, n, start, 0)

    def fill(k, c):
        own = source[p * w + k] - p * w
        inside = (own >= 0) & (own < w)
        final[0, k] = jnp.where(inside, own, 0)
        final[1, k] = -1
        return c

    lax.fori_loop(0, w, fill, 0)

    def listing(cut, going_right, worst):
        into = right if going_right else left
        arriving = (p == cut + 1) if going_right else (p == cut)
        leaving = (p == cut) if going_right else (p == cut + 1)

        def by_distance(e, count):
            reach = planes - 1 - e if going_right else e

            def add(s, count):
                at = s // w
                if going_right:
                    hit = (at <= cut) & (far_r[s] == reach) & (reach > cut)
                else:
                    hit = (at > cut) & (far_l[s] == reach) & (reach <= cut)

                @pl.when(hit & leaving)
                def _():
                    relayed = at != p
                    into[0, count] = jnp.where(relayed, 0, s - p * w)
                    into[1, count] = jnp.where(relayed, before[s], -1)

                @pl.when(hit & arriving)
                def _():
                    before[s] = count

                    def serve(k, c):
                        @pl.when(source[p * w + k] == s)
                        def _():
                            final[1, k] = 2 * count + (0 if going_right else 1)

                        return c

                    lax.fori_loop(0, w, serve, 0)

                return count + jnp.where(hit, 1, 0)

            return lax.fori_loop(0, n, add, count)

        steps = planes - 1
        count = lax.fori_loop(0, steps, by_distance, jnp.int32(0))
        return jnp.maximum(worst, count)

    worst = lax.fori_loop(0, planes - 1, lambda c, m: listing(c, True, m), jnp.int32(0))
    worst = lax.fori_loop(0, planes - 1, lambda c, m: listing(planes - 2 - c, False, m), worst)
    need[0] = worst


def kernel(n, w, cap, *refs):
    (source, order, right, left, final, lengths, bc_cols, dt_bias, d_skip) = refs[:9]
    (cache, pool_k, pool_v, q_hbm, sk_hbm, sv_hbm, u_hbm, dt_hbm, a_hbm) = refs[9:18]
    (mamba_hbm, attn_hbm, final_hbm) = refs[18:21]
    (held_s, held_k, held_v, send_s, send_k, send_v, got_s, got_k, got_v) = refs[21:30]
    (keys, values, q_v, u_v, dt_v, a_v, mamba_v, attn_v, final_v) = refs[30:39]
    (delta_w, du_w, y_w, h_w, rate_w, bc_w, w_w, inv_w) = refs[39:47]
    (send_sem, recv_sem, own_sem, in_sem, out_sem) = refs[47:52]
    if cap:
        (hop_send, hop_recv) = refs[52:54]
        boxes = refs[54:]
    me = lax.axis_index("req")
    p = lax.div(me, w)
    mine = lax.rem(me, w)
    planes = n // w
    tokens, channels = u_v.shape
    nstate = a_v.shape[0]
    blocks = channels // WIDE
    width = held_s.shape[2]
    total = keys.shape[0]
    prefix_len = total - tokens
    chunks, size, _ = got_k.shape
    per = chunks // w
    heads = q_v.shape[1] // HD
    q_group = heads // (keys.shape[1] // HD)

    def box(kind, outward, way, k):
        return boxes[((kind * 2 + outward) * 2 + way) * cap + k]

    loads = [
        pltpu.make_async_copy(dt_hbm, dt_v, in_sem.at[0]),
        pltpu.make_async_copy(u_hbm, u_v, in_sem.at[1]),
        pltpu.make_async_copy(a_hbm, a_v, in_sem.at[2]),
        pltpu.make_async_copy(q_hbm, q_v, in_sem.at[3]),
        pltpu.make_async_copy(sk_hbm, keys.at[pl.ds(prefix_len, tokens)], in_sem.at[4]),
        pltpu.make_async_copy(sv_hbm, values.at[pl.ds(prefix_len, tokens)], in_sem.at[5]),
    ]
    for load in loads:
        load.start()

    barrier = pltpu.get_barrier_semaphore()
    sides = (p < planes - 1, p > 0)

    def greet(peer):
        pl.semaphore_signal(barrier, inc=1, device_id={"req": peer}, device_id_type=MESH)

    def greet_step(d, c):
        greet(p * w + lax.rem(mine + d, w))
        return c

    lax.fori_loop(1, w, greet_step, 0)
    for way in range(2 if cap else 0):

        @pl.when(jnp.logical_not(sides[1 - way]))
        def _():
            for kind in range(3):
                for k in range(cap):
                    ref = box(kind, 0, way, k)
                    ref[...] = jnp.zeros_like(ref)

        @pl.when(sides[way])
        def _():
            greet(me + w if way == 0 else me - w)

    near = sides[0].astype(jnp.int32) + sides[1].astype(jnp.int32) if cap else 0
    pl.semaphore_wait(barrier, w - 1 + near)

    def part(kind, index):
        if kind == 0:
            return cache.at[:, pl.ds(pl.multiple_of(index * width, width), width)]
        pool = pool_k if kind == 1 else pool_v
        return pool.at[pl.ds(index * per, per)]

    held = (held_s, held_k, held_v)
    outgoing = (send_s, send_k, send_v)
    got = (got_s, got_k, got_v)

    def spread(kind):
        own = pltpu.make_async_copy(part(kind, mine), held[kind].at[mine], own_sem.at[kind])
        own.start()

        def step(d, c):
            other = lax.rem(mine + d, w)
            pltpu.make_async_remote_copy(
                src_ref=part(kind, other),
                dst_ref=held[kind].at[mine],
                send_sem=send_sem.at[kind],
                recv_sem=recv_sem.at[kind],
                device_id={"req": p * w + other},
                device_id_type=MESH,
            ).start()
            return c

        lax.fori_loop(1, w, step, 0)

    def settle(ref, sem):
        piece = ref.at[pl.ds(0, ref.shape[0] // w * (w - 1))]
        pltpu.make_async_copy(piece, piece, sem).wait()

    def gathered(kind):
        settle(held[kind], recv_sem.at[kind])
        pltpu.make_async_copy(part(kind, mine), held[kind].at[mine], own_sem.at[kind]).wait()

    def crossing(kind, way, k):
        return pltpu.make_async_remote_copy(
            src_ref=box(kind, 1, way, k),
            dst_ref=box(kind, 0, way, k),
            send_sem=hop_send.at[(kind * 2 + way) * cap + k],
            recv_sem=hop_recv.at[(kind * 2 + way) * cap + k],
            device_id={"req": me + w if way == 0 else me - w},
            device_id_type=MESH,
        )

    def hop(kind, k):
        for way in range(2):
            table = (right, left)[way]

            @pl.when(sides[1 - way])
            def _():
                crossing(kind, way, k).wait_recv()

            @pl.when(sides[way])
            def _():
                item = held[kind][table[0, k]]
                code = table[1, k]
                for e in range(k + 1):
                    item = jnp.where(code == e, box(kind, 0, way, e)[...], item)
                box(kind, 1, way, k)[...] = item
                crossing(kind, way, k).start()

    def deliver(kind):
        def choose(r):
            item = held[kind][final[0, r]]
            code = final[1, r]
            for e in range(cap):
                for way in range(2):
                    item = jnp.where(code == 2 * e + way, box(kind, 0, way, e)[...], item)
            return item

        def pick(r, c):
            outgoing[kind][r] = choose(r)
            return c

        lax.fori_loop(0, w, pick, 0)
        if kind == 0:
            landing = got_s.at[mine]
            got_s[mine] = choose(mine)
        else:
            landing = got[kind].at[pl.ds(mine * per, per)]
            got[kind][pl.ds(mine * per, per)] = choose(mine)

        def step(d, c):
            other = lax.rem(mine + d, w)
            pltpu.make_async_remote_copy(
                src_ref=outgoing[kind].at[other],
                dst_ref=landing,
                send_sem=send_sem.at[3 + kind],
                recv_sem=recv_sem.at[3 + kind],
                device_id={"req": p * w + other},
                device_id_type=MESH,
            ).start()
            return c

        lax.fori_loop(1, w, step, 0)

    spread(0)
    spread(1)
    if cap:
        spread(2)

    def widen(k, c):
        bc_w[k] = jnp.broadcast_to(bc_cols[k], (tokens, LANE))
        return c

    lax.fori_loop(0, 2 * nstate, widen, 0)

    length = lengths[0]
    live = lax.broadcasted_iota(jnp.int32, (tokens, LANE), 0) < length
    loads[0].wait()
    loads[1].wait()

    def steps_of(b, c):
        for s in range(SUB):
            at = pl.ds(pl.multiple_of(b * WIDE + s * LANE, LANE), LANE)
            raw = dt_v[:, at].astype(jnp.float32) + dt_bias[:, at]
            soft = jnp.maximum(raw, 0.0) + jnp.log1p(jnp.exp(-jnp.abs(raw)))
            delta = jnp.where(live, soft, 0.0)
            delta_w[b, pl.ds(s, tokens, stride=SUB), :] = delta
            du_w[b, pl.ds(s, tokens, stride=SUB), :] = delta * u_v[:, at].astype(jnp.float32)
        return c

    lax.fori_loop(0, blocks, steps_of, 0)
    gathered(0)
    for k in range(cap):
        hop(0, k)
    deliver(0)
    if not cap:
        spread(2)
    loads[2].wait()

    def rates_of(b, c):
        for s in range(SUB):
            at = pl.ds(pl.multiple_of(b * WIDE + s * LANE, LANE), LANE)
            rate_w[b, pl.ds(s, nstate, stride=SUB), :] = -LOG2E * jnp.exp(a_v[:, at])
        return c

    lax.fori_loop(0, blocks, rates_of, 0)
    gathered(1)
    later = [functools.partial(hop, 1, k) for k in range(cap)] + [functools.partial(deliver, 1)]
    later += [functools.partial(gathered, 2)] + [functools.partial(hop, 2, k) for k in range(cap)]
    later += [functools.partial(deliver, 2)]
    if cap:
        later.pop(0)()
    else:
        later.pop(0)()
    settle(got_s, recv_sem.at[3])

    def scan_block(b, c):
        for s in range(SUB):
            first = b * WIDE + s * LANE
            inside = lax.rem(first, width)
            start = got_s[lax.div(first, width), :, pl.ds(pl.multiple_of(inside, LANE), LANE)]
            h_w[pl.ds(s, nstate, stride=SUB), :] = start.astype(jnp.float32)
        rates = [rate_w[b, pl.ds(k * SUB, SUB), :] for k in range(nstate)]

        def advance(t, hs):
            at = pl.ds(pl.multiple_of(t * SUB, SUB), SUB)
            delta = delta_w[b, at, :]
            du = du_w[b, at, :]
            new = []
            sums = [None, None]
            for k in range(nstate):
                h = jnp.exp2(delta * rates[k]) * hs[k] + du * bc_w[k, pl.ds(t, 1), :]
                term = bc_w[nstate + k, pl.ds(t, 1), :] * h
                sums[k % 2] = term if sums[k % 2] is None else sums[k % 2] + term
                new.append(h)
            y_w[at, :] = sums[0] + sums[1]
            return tuple(new)

        def pair(i, hs):
            return advance(2 * i + 1, advance(2 * i, hs))

        hs = tuple(h_w[pl.ds(k * SUB, SUB), :] for k in range(nstate))
        hs = lax.fori_loop(0, tokens // 2, pair, hs)
        for k in range(nstate):
            h_w[pl.ds(k * SUB, SUB), :] = hs[k]
        for s in range(SUB):
            at = pl.ds(pl.multiple_of(b * WIDE + s * LANE, LANE), LANE)
            final_v[:, at] = h_w[pl.ds(s, nstate, stride=SUB), :]
            y = y_w[pl.ds(s, tokens, stride=SUB), :] + d_skip[:, at] * u_v[:, at].astype(jnp.float32)
            mamba_v[:, at] = jnp.where(live, y, 0.0).astype(jnp.bfloat16)
        return c

    at_once = 1 if cap else 4
    for first in range(0, blocks, at_once):
        lax.fori_loop(first, min(first + at_once, blocks), scan_block, 0)
        if later and first + at_once < blocks:
            later.pop(0)()
            if later and later[0].func is gathered:
                later.pop(0)()
    if not cap:
        for job in later:
            job()
        later = []

    stores = [
        pltpu.make_async_copy(mamba_v, mamba_hbm, out_sem.at[0]),
        pltpu.make_async_copy(final_v, final_hbm, out_sem.at[1]),
        pltpu.make_async_copy(attn_v, attn_hbm, out_sem.at[2]),
    ]
    stores[0].start()
    stores[1].start()

    def arrange(kind, into):
        def step(k, c):
            to = pl.ds(pl.multiple_of(k * size, size), size)
            into[to, :] = got[kind][order[lax.div(k, fine)] * fine + lax.rem(k, fine)]
            return c

        fine = chunks // order.shape[0]
        lax.fori_loop(0, chunks, step, 0)

    loads[3].wait()
    loads[4].wait()
    while later and not (later[0].func is hop and later[0].args[0] == 2):
        later.pop(0)()
    settle(got_k, recv_sem.at[4])
    arrange(1, keys)
    factor = LOG2E / math.sqrt(HD)
    row = lax.broadcasted_iota(jnp.int32, (tokens, tokens), 0)
    col = lax.broadcasted_iota(jnp.int32, (tokens, tokens), 1)

    def weigh(j):
        g = lax.div(j, q_group)
        q = q_v[:, pl.ds(pl.multiple_of(j * HD, HD), HD)]
        k = keys[:, pl.ds(pl.multiple_of(g * HD, HD), HD)]
        scores = lax.dot_general(q, k, (((1,), (1,)), ((), ())), preferred_element_type=jnp.float32)
        scores = jnp.concatenate(
            [
                jnp.where(col > row, scores[:, :tokens], -1e30),
                scores[:, tokens:prefix_len],
                jnp.where(col <= row, scores[:, prefix_len:], -1e30),
            ],
            axis=1,
        )
        highest = jnp.max(scores, axis=1, keepdims=True)
        weight = jnp.exp2((scores - highest) * factor)
        inv_w[j] = jnp.broadcast_to(1.0 / jnp.sum(weight, axis=1, keepdims=True), (tokens, HD))
        w_w[j] = weight.astype(jnp.bfloat16)

    def weigh_pair(i, c):
        weigh(2 * i)
        weigh(2 * i + 1)
        return c

    lots = len(later)
    bounds = [heads // 2 * e // (lots + 1) for e in range(lots + 2)]
    for first, last in zip(bounds, bounds[1:]):
        lax.fori_loop(first, last, weigh_pair, 0)
        if later:
            later.pop(0)()
    while later:
        later.pop(0)()

    loads[5].wait()
    settle(got_v, recv_sem.at[5])
    arrange(2, values)

    def mix(j):
        g = lax.div(j, q_group)
        v = values[:, pl.ds(pl.multiple_of(g * HD, HD), HD)]
        out = jnp.dot(w_w[j], v, preferred_element_type=jnp.float32) * inv_w[j]
        out = jnp.where(live, out, 0.0)
        attn_v[:, pl.ds(pl.multiple_of(j * HD, HD), HD)] = out.astype(jnp.bfloat16)

    def mix_pair(i, c):
        mix(2 * i)
        mix(2 * i + 1)
        return c

    lax.fori_loop(0, heads // 2, mix_pair, 0)
    stores[2].start()
    for kind in range(3):
        settle(held[kind], send_sem.at[kind])
        settle(outgoing[kind], send_sem.at[3 + kind])
        for k in range(cap):
            for way in range(2):

                @pl.when(sides[way])
                def _():
                    crossing(kind, way, k).wait_send()

    for store in stores:
        store.wait()


def solution(mesh):
    n, groups = mesh.shape["req"], mesh.shape["groups"]

    def local(
        cache_states,
        pool_keys,
        pool_values,
        slot_prefix,
        page_table,
        prefix_id,
        lengths,
        queries,
        suffix_keys,
        suffix_values,
        u_in,
        dt_raw,
        bc_in,
        a_log,
        dt_bias,
        d_skip,
    ):
        nstate, channels = a_log.shape
        tokens = u_in.shape[0]
        kv = suffix_keys.shape[1]
        prefix_len = pool_keys.shape[0] * pool_keys.shape[1]
        heads = queries.shape[1] // HD
        blocks = channels // WIDE
        bf, f32 = jnp.bfloat16, jnp.float32
        smem = pl.BlockSpec(memory_space=pltpu.SMEM)
        vmem = pl.BlockSpec(memory_space=pltpu.VMEM)
        hbm = pl.BlockSpec(memory_space=pl.ANY)
        total = prefix_len + tokens
        page_count, page = pool_keys.shape[:2]
        plane = 1
        while plane * plane * 4 <= n:
            plane *= 2
        plane = plane if n % plane == 0 else n
        plane = min(plane, n)

        def ints(*shape):
            return jax.ShapeDtypeStruct(shape, jnp.int32)

        me = lax.axis_index("req").astype(jnp.int32).reshape(1)
        source, order, right, left, final_plan, need = pl.pallas_call(
            functools.partial(plan_kernel, n, plane),
            out_shape=(ints(n), ints(page_count), ints(2, n), ints(2, n), ints(2, n), ints(1)),
            in_specs=[smem] * 4,
            out_specs=(smem,) * 6,
            scratch_shapes=[pltpu.SMEM((n,), jnp.int32)] * 3,
        )(slot_prefix, prefix_id, page_table, me)
        shift = 1
        while shift < groups:
            ring = [(g, (g + shift) % groups) for g in range(groups)]
            need = jnp.maximum(need, lax.ppermute(need, "groups", ring))
            shift *= 2

        def build(w, cap, number):
            size = min(page, prefix_len // w)
            chunks = prefix_len // size
            per = chunks // w
            width = channels // w
            state = (nstate, width)
            piece = (per, size, kv)
            item = [pltpu.VMEM(state, bf)] * (4 * cap) + [pltpu.VMEM(piece, bf)] * (8 * cap)
            hops = [pltpu.SemaphoreType.DMA((6 * cap,))] * 2 + item if cap else []
            scratch = (
                ([pltpu.VMEM((w, *state), bf)] + [pltpu.VMEM((w, *piece), bf)] * 2) * 2
                + [pltpu.VMEM((w, *state), bf)]
                + [pltpu.VMEM((chunks, size, kv), bf)] * 2
                + [
                    pltpu.VMEM((total, kv), bf),
                    pltpu.VMEM((total, kv), bf),
                    pltpu.VMEM(queries.shape, bf),
                    pltpu.VMEM(u_in.shape, bf),
                    pltpu.VMEM(dt_raw.shape, bf),
                    pltpu.VMEM(a_log.shape, f32),
                    pltpu.VMEM(u_in.shape, bf),
                    pltpu.VMEM(queries.shape, bf),
                    pltpu.VMEM(a_log.shape, f32),
                    pltpu.VMEM((blocks, tokens * SUB, LANE), f32),
                    pltpu.VMEM((blocks, tokens * SUB, LANE), f32),
                    pltpu.VMEM((tokens * SUB, LANE), f32),
                    pltpu.VMEM((nstate * SUB, LANE), f32),
                    pltpu.VMEM((blocks, nstate * SUB, LANE), f32),
                    pltpu.VMEM((2 * nstate, tokens, LANE), f32),
                    pltpu.VMEM((heads, tokens, total), bf),
                    pltpu.VMEM((heads, tokens, HD), f32),
                    pltpu.SemaphoreType.DMA((6,)),
                    pltpu.SemaphoreType.DMA((6,)),
                    pltpu.SemaphoreType.DMA((3,)),
                    pltpu.SemaphoreType.DMA((6,)),
                    pltpu.SemaphoreType.DMA((3,)),
                ]
                + hops
            )

            def run(*args):
                (source, final_plan, order, right, left, pool_keys, pool_values, *rest) = args
                final_plan = final_plan if cap else jnp.stack([source, jnp.full_like(source, -1)])
                pools = (pool_keys.reshape(chunks, size, kv), pool_values.reshape(chunks, size, kv))
                return pl.pallas_call(
                    functools.partial(kernel, n, w, cap),
                    out_shape=(
                        jax.ShapeDtypeStruct(u_in.shape, bf),
                        jax.ShapeDtypeStruct(queries.shape, bf),
                        jax.ShapeDtypeStruct(a_log.shape, f32),
                    ),
                    in_specs=[smem] * 6 + [vmem] * 3 + [hbm] * 9,
                    out_specs=(hbm, hbm, hbm),
                    scratch_shapes=scratch,
                    compiler_params=pltpu.CompilerParams(
                        collective_id=number, has_side_effects=True, vmem_limit_bytes=64 * 1000 * 1024
                    ),
                )(source, order, right, left, final_plan, *rest[:5], *pools, *rest[5:])

            return run

        args = (
            source,
            final_plan,
            order,
            right,
            left,
            pool_keys,
            pool_values,
            lengths,
            bc_in[0][:, :, None],
            dt_bias[None],
            d_skip[None],
            cache_states[0],
            queries,
            suffix_keys,
            suffix_values,
            u_in,
            dt_raw,
            a_log,
        )
        caps = CAPS
        choices = [build(plane, cap, e) for e, cap in enumerate(caps)] + [build(n, 0, len(caps))]
        which = sum((need[0] > cap).astype(jnp.int32) for cap in caps)
        mamba, attn, final = lax.switch(which, choices, *args)
        return mamba, attn, final[None]

    split = ("groups", "req")
    one, two, three = P(split), P(split, None), P(split, None, None)
    return jax.shard_map(
        local,
        mesh=mesh,
        in_specs=(
            three,
            three,
            three,
            P("groups"),
            P("groups", None),
            P("groups"),
            one,
            two,
            two,
            two,
            two,
            two,
            three,
            P(),
            P(),
            P(),
        ),
        out_specs=(two, two, three),
        check_vma=False,
    )
```

time: 130 us -> 437 us (3.36); the launches traced: 129 us -> 431 us
  Pallas kernels: 115 us -> 418 us
    pallas_call x1 -> x2, Pallas kernels: 115 us -> 418 us  [the longest x1 409 us: run(): pl.pallas_call(functools.partial(kernel, n, w, cap), out_shape=(jax.Shape...]
  transfers between devices with their start and end apart: 0 -> 1, of which waited for: 0 -> 1; matrix products, arithmetic and copies ran while one was open for 0% -> 0% of each run, Pallas kernels for 0% -> 0%
where the time goes in v2:
time: 437 us; the launch traced here: 431 us
  Pallas kernels  418 us (96%)
  local copies, waits for them, and re-layouts  7.8 us (2%)
    pallas_call x1, Pallas kernels, run(): pl.pallas_call(functools.partial(kernel, n, w, cap), out_shape=(jax.Shape...  409 us
    pallas_call x1, Pallas kernels, local(): pl.pallas_call(functools.partial(plan_kernel, n, plane), out_shape=(ints(...  9.24 us
  transfers between devices with their start and end apart: 1, of which 1 were waited for; matrix products, arithmetic and copies ran while one was open for 0% of the time, Pallas kernels for 0%

profile of v2, /device:TPU:13, one launch (start us, length us, event | category | flops | bytes accessed | tf_op | source)
XLA Modules:
  0.0 430.7 jit_solution(16892691918297912254)
XLA Ops:
  0.6 9.2 %shard_map.179 = (s32[16]{0:T(128)}, s32[16]{0:T(128)}, s32[2,16]{1,0:T(2,128)}, s32[2,16]{1,0:T(2,128)}, s32[2,16]{1,0:T(2,128)}, /*index=5*/s32[1]{0:T(128)}) custom-call(s32[16]{0:T(128)} %slot_prefix.1, s32[16]{0:T(128)} %prefix_id.1, s32[16,16]{1,0:T(8,128)} %page_table.1, s32[1]{0:T(128)} %bitcast.5.where_ref), custom_call_target="tpu_custom_call" | custom-call | tf_op jit(solution)/shard_map/pallas_call | solution.py:518
  9.9 1.2 collective-permute-start
  11.1 1.4 collective-permute-done
  13.8 411.9 %conditional.1 = (bf16[128,8192]{1,0:T(8,128)(2,1)}, bf16[128,4096]{1,0:T(8,128)(2,1)}, f32[1,16,8192]{2,1,0:T(8,128)}) conditional(s32[]{:T(128)} %bitcast.6, (s32[16]{0:T(128)}, s32[16]{0:T(128)}, s32[2,16]{1,0:T(2,128)}, s32[2,16]{1,0:T(2,128)}, s32[2,16]{1,0:T(2,128)}, /*index=5*/s32[1]{0:T(128)}, ...), branch_computations={%region_0.0_spmd, %region_1.0_spmd, %region_2.0_spmd, %region_3.0_... | conditional | bytes 6062440 | solution.py:615
  13.8 0.0 copy-start.1
  13.8 0.0 copy-start.5
  13.9 0.0 copy-start.9
  13.9 0.0 copy-start.14
  13.9 0.0 copy-start.18
  13.9 2.8 copy.24.refs_6_
  16.7 0.0 copy-done.1
  16.7 0.0 copy-done.5
  16.7 0.0 copy-done.9
  16.7 0.0 copy-done.14
  16.7 0.0 copy-done.18
  16.7 408.8 %branch_1_fun.1 = (bf16[128,8192]{1,0:T(8,128)(2,1)}, bf16[128,4096]{1,0:T(8,128)(2,1)}, f32[16,8192]{1,0:T(8,128)}) custom-call(s32[16]{0:T(128)} %get-tuple-element.176.refs_0_, s32[16]{0:T(128)} %get-tuple-element.177.refs_1_, s32[2,16]{1,0:T(2,128)} %get-tuple-element.178.refs_2_, s32[2,16]{1,0:T(2,128)} %get-tuple-element.179.refs_3_, ...), custom_call_target="tpu_custom_call" | custom-call | tf_op jit(solution)/shard_map/cond/branch_1_fun/pallas_call | solution.py:575
  425.7 0.0 copy-start.12
  425.7 0.0 copy-start.21
  425.7 3.2 copy.42
  428.9 0.0 copy-done.12
  428.9 1.0 copy.43
  429.9 0.0 copy-done.21
  429.9 0.8 copy.44
Async XLA Ops:
  9.9 2.6 collective-permute-start
  13.8 2.8 copy-start.1
  13.8 2.8 copy-start.5
  13.9 2.8 copy-start.9
  13.9 2.8 copy-start.14
  13.9 2.8 copy-start.18
  425.7 3.2 copy-start.12
  425.7 4.2 copy-start.21
